TPU v7x, 32 devices: a whole 2x2x4 slice. The times are simulated.
32 devices in a mesh: rep: 16 (over z, x, core), slab: 2 (over y).
Axes of the slice: x: 2, y: 2, z: 4, core: 2. Of those that a mesh axis runs over, the one named last changes fastest.
Arguments:
- weights: bfloat16 [16, 256, 3072], P('rep', 'slab'), may hold values from -6 to 6
- perms: int32 [16, 8, 256], P('rep'), may hold values from 0 to 255, each once within a row
Outputs:
- merged: bfloat16 [16, 256, 3072], P('rep', 'slab')
Inputs may be any that keep to these rules, and one draw needn't show every extreme that they name: `perms`: each row of 256 entries names every neuron of the window once.
All inputs are finite; a program needn't handle non-finite values.
Results may differ from a plain program's by a relative error of at most 0.012.
Values may be sent and summed in bfloat16 or wider, within the bound.
A program may use at most 64 MiB of HBM per device.

v0:
```python
import math
import jax
import jax.numpy as jnp
from jax import lax
from jax.sharding import PartitionSpec as P

D = 3072
ROUNDS = 8


def from_partner(x, axis, stride):
    return lax.ppermute(x, axis, [(i, i ^ 1 << stride) for i in range(lax.axis_size(axis))])


def finish_round(own, partner, perm_rows, cost):
    squared = cost * cost
    fourth = squared * squared
    soft_plan = fourth / (1.0 + jnp.sum(fourth, axis=1, keepdims=True))
    columns = jnp.arange(partner.shape[0], dtype=jnp.int32)
    onehot = (perm_rows[:, None] == columns[None, :]).astype(jnp.float32)
    mixing = (onehot + soft_plan).astype(jnp.bfloat16)
    aligned = 0.5 * jnp.dot(mixing, partner, preferred_element_type=jnp.float32)
    return ((own.astype(jnp.float32) + aligned) * (1.0 / math.sqrt(2.0))).astype(jnp.bfloat16)


def local(weights, perms):
    bit_count = lax.axis_size("rep").bit_length() - 1
    current = weights[0]
    perm_plan = perms[0]
    feature_part = lax.all_to_all(current, "slab", split_axis=1, concat_axis=0, tiled=True)
    for round_idx in range(ROUNDS):
        partner = from_partner(feature_part, "rep", round_idx % bit_count)
        partial_value = jnp.dot(feature_part, partner.T, preferred_element_type=jnp.float32)
        cost = lax.psum(partial_value, "slab") * (1.0 / math.sqrt(D))
        feature_part = finish_round(feature_part, partner, perm_plan[round_idx], cost)
    result = lax.all_to_all(feature_part, "slab", split_axis=0, concat_axis=1, tiled=True)
    return result[None]


def solution(mesh):
    placed = (P("rep", "slab", None), P("rep", None, None))
    return jax.shard_map(
        local, mesh=mesh, in_specs=placed, out_specs=P("rep", "slab", None), check_vma=False
    )
```

profile of v0, /device:TPU:0, one launch (start us, length us, event | category | flops | bytes accessed | tf_op | source)
XLA Modules:
  0.0 416.3 jit_solution(1840238187815374392)
XLA Ops:
  6.5 2.6 all_to_all.26
  9.2 14.8 %all_to_all.35 = bf16[128,2,1536]{2,0,1:T(8,128)(2,1)S(1)} all-to-all(bf16[128,2,1536]{2,0,1:T(8,128)(2,1)S(1)} %copy.3), channel_id=1, replica_groups=mesh['rep'=16,'slab'=2] {'slab'}, dimensions={1} | all-to-all | bytes 1572864 | tf_op jit(solution)/shard_map/all_to_all | solution.py:30
  24.0 2.3 collective-permute-done
  27.5 23.8 %all-reduce.9.cloned.1.call-done = f32[256,256]{1,0:T(8,128)} async-done(((f32[256,256]{1,0:T(8,128)}), f32[256,256]{1,0:T(8,128)}) %all-reduce.9.cloned.1.call-update) | async-done | bytes 262160 | tf_op jit(solution)/shard_map/psum | solution.py:34
  52.4 1.4 fusion.16
  53.8 1.5 collective-permute-start.1
  55.4 17.3 %collective-permute-done.1 = bf16[256,1536]{1,0:T(8,128)(2,1)S(1)} collective-permute-done((bf16[256,1536]{1,0:T(8,128)(2,1)S(1)}, bf16[256,1536]{1,0:T(8,128)(2,1)S(1)}, u32[]{:S(2)}, u32[]{:S(2)}) %collective-permute-start.1) | collective-permute-done | bytes 786464 | tf_op jit(solution)/shard_map/ppermute | solution.py:12
  73.8 23.4 %all-reduce.11.cloned.1.call-done = f32[256,256]{1,0:T(8,128)} async-done(((f32[256,256]{1,0:T(8,128)}), f32[256,256]{1,0:T(8,128)}) %all-reduce.11.cloned.1.call-update) | async-done | bytes 262160 | tf_op jit(solution)/shard_map/psum | solution.py:34
  98.3 1.4 fusion.17
  99.7 1.6 collective-permute-start.2
  101.3 17.3 %collective-permute-done.2 = bf16[256,1536]{1,0:T(8,128)(2,1)S(1)} collective-permute-done((bf16[256,1536]{1,0:T(8,128)(2,1)S(1)}, bf16[256,1536]{1,0:T(8,128)(2,1)S(1)}, u32[]{:S(2)}, u32[]{:S(2)}) %collective-permute-start.2) | collective-permute-done | bytes 786464 | tf_op jit(solution)/shard_map/ppermute | solution.py:12
  119.8 23.4 %all-reduce.13.cloned.1.call-done = f32[256,256]{1,0:T(8,128)} async-done(((f32[256,256]{1,0:T(8,128)}), f32[256,256]{1,0:T(8,128)}) %all-reduce.13.cloned.1.call-update) | async-done | bytes 262160 | tf_op jit(solution)/shard_map/psum | solution.py:34
  144.2 1.4 fusion.18
  145.7 2.5 collective-permute-start.3
  148.1 34.1 %collective-permute-done.3 = bf16[256,1536]{1,0:T(8,128)(2,1)S(1)} collective-permute-done((bf16[256,1536]{1,0:T(8,128)(2,1)S(1)}, bf16[256,1536]{1,0:T(8,128)(2,1)S(1)}, u32[]{:S(2)}, u32[]{:S(2)}) %collective-permute-start.3) | collective-permute-done | bytes 786464 | tf_op jit(solution)/shard_map/ppermute | solution.py:12
  183.4 23.4 %all-reduce.15.cloned.1.call-done = f32[256,256]{1,0:T(8,128)} async-done(((f32[256,256]{1,0:T(8,128)}), f32[256,256]{1,0:T(8,128)}) %all-reduce.15.cloned.1.call-update) | async-done | bytes 262160 | tf_op jit(solution)/shard_map/psum | solution.py:34
  207.9 1.4 fusion.19
  209.4 2.3 collective-permute-done.4
  212.8 23.4 %all-reduce.17.cloned.1.call-done = f32[256,256]{1,0:T(8,128)} async-done(((f32[256,256]{1,0:T(8,128)}), f32[256,256]{1,0:T(8,128)}) %all-reduce.17.cloned.1.call-update) | async-done | bytes 262160 | tf_op jit(solution)/shard_map/psum | solution.py:34
  237.3 1.4 fusion.20
  238.7 1.5 collective-permute-start.5
  240.3 17.3 %collective-permute-done.5 = bf16[256,1536]{1,0:T(8,128)(2,1)S(1)} collective-permute-done((bf16[256,1536]{1,0:T(8,128)(2,1)S(1)}, bf16[256,1536]{1,0:T(8,128)(2,1)S(1)}, u32[]{:S(2)}, u32[]{:S(2)}) %collective-permute-start.5) | collective-permute-done | bytes 786464 | tf_op jit(solution)/shard_map/ppermute | solution.py:12
  258.8 23.4 %all-reduce.19.cloned.1.call-done = f32[256,256]{1,0:T(8,128)} async-done(((f32[256,256]{1,0:T(8,128)}), f32[256,256]{1,0:T(8,128)}) %all-reduce.19.cloned.1.call-update) | async-done | bytes 262160 | tf_op jit(solution)/shard_map/psum | solution.py:34
  284.7 1.6 collective-permute-start.6
  286.2 17.3 %collective-permute-done.6 = bf16[256,1536]{1,0:T(8,128)(2,1)S(1)} collective-permute-done((bf16[256,1536]{1,0:T(8,128)(2,1)S(1)}, bf16[256,1536]{1,0:T(8,128)(2,1)S(1)}, u32[]{:S(2)}, u32[]{:S(2)}) %collective-permute-start.6) | collective-permute-done | bytes 786464 | tf_op jit(solution)/shard_map/ppermute | solution.py:12
  304.7 23.4 %all-reduce.21.cloned.1.call-done = f32[256,256]{1,0:T(8,128)} async-done(((f32[256,256]{1,0:T(8,128)}), f32[256,256]{1,0:T(8,128)}) %all-reduce.21.cloned.1.call-update) | async-done | bytes 262160 | tf_op jit(solution)/shard_map/psum | solution.py:34
  330.6 2.5 collective-permute-start.7
  333.1 34.1 %collective-permute-done.7 = bf16[256,1536]{1,0:T(8,128)(2,1)S(1)} collective-permute-done((bf16[256,1536]{1,0:T(8,128)(2,1)S(1)}, bf16[256,1536]{1,0:T(8,128)(2,1)S(1)}, u32[]{:S(2)}, u32[]{:S(2)}) %collective-permute-start.7) | collective-permute-done | bytes 786464 | tf_op jit(solution)/shard_map/ppermute | solution.py:12
  368.3 23.4 %all-reduce.23.cloned.1.call-done = f32[256,256]{1,0:T(8,128)} async-done(((f32[256,256]{1,0:T(8,128)}), f32[256,256]{1,0:T(8,128)}) %all-reduce.23.cloned.1.call-update) | async-done | bytes 262160 | tf_op jit(solution)/shard_map/psum | solution.py:34
  392.8 1.4 fusion.23
  394.2 13.0 %all_to_all.36 = bf16[2,128,1536]{2,1,0:T(8,128)(2,1)S(1)} all-to-all(bf16[2,128,1536]{2,1,0:T(8,128)(2,1)S(1)} %bitcast.41), channel_id=1, replica_groups=mesh['rep'=16,'slab'=2] {'slab'}, dimensions={0} | all-to-all | bytes 1572864 | tf_op jit(solution)/shard_map/all_to_all | solution.py:36
  408.0 1.5 broadcast_in_dim.2
  (49 shorter events, 21.6 us)
Async XLA Ops:
  6.5 44.8 %all-reduce.9.cloned.1.call-start = ((), (), s32[]{:S(2)}) async-start(), calls=%async_computation.2 | async-start | bytes 524288 | tf_op jit(solution)/shard_map/psum | solution.py:34
  24.0 3.5 copy-start
  24.0 2.3 collective-permute-start
  27.5 69.8 %all-reduce.11.cloned.1.call-start = ((), (), s32[]{:S(2)}) async-start(), calls=%async_computation.3 | async-start | bytes 524288 | tf_op jit(solution)/shard_map/psum | solution.py:34
  53.8 18.8 %collective-permute-start.1 = (bf16[256,1536]{1,0:T(8,128)(2,1)S(1)}, bf16[256,1536]{1,0:T(8,128)(2,1)S(1)}, u32[]{:S(2)}, u32[]{:S(2)}) collective-permute-start(bf16[256,1536]{1,0:T(8,128)(2,1)S(1)} %fusion.16), channel_id=1, source_target_pairs={{0,4},{2,6},{4,0},{6,2},{8,12},{10,14},{12,8},{14,10},{16,20},{18,... | collective-permute-start | bytes 2359304 | tf_op jit(solution)/shard_map/ppermute | solution.py:12
  73.8 69.4 %all-reduce.13.cloned.1.call-start = ((), (), s32[]{:S(2)}) async-start(), calls=%async_computation.4 | async-start | bytes 524288 | tf_op jit(solution)/shard_map/psum | solution.py:34
  99.7 18.8 %collective-permute-start.2 = (bf16[256,1536]{1,0:T(8,128)(2,1)S(1)}, bf16[256,1536]{1,0:T(8,128)(2,1)S(1)}, u32[]{:S(2)}, u32[]{:S(2)}) collective-permute-start(bf16[256,1536]{1,0:T(8,128)(2,1)S(1)} %fusion.17), channel_id=1, source_target_pairs={{0,8},{2,10},{4,12},{6,14},{8,0},{10,2},{12,4},{14,6},{16,24},{18,... | collective-permute-start | bytes 2359304 | tf_op jit(solution)/shard_map/ppermute | solution.py:12
  119.7 87.1 %all-reduce.15.cloned.1.call-start = ((), (), s32[]{:S(2)}) async-start(), calls=%async_computation.5 | async-start | bytes 524288 | tf_op jit(solution)/shard_map/psum | solution.py:34
  145.7 36.6 %collective-permute-start.3 = (bf16[256,1536]{1,0:T(8,128)(2,1)S(1)}, bf16[256,1536]{1,0:T(8,128)(2,1)S(1)}, u32[]{:S(2)}, u32[]{:S(2)}) collective-permute-start(bf16[256,1536]{1,0:T(8,128)(2,1)S(1)} %fusion.18), channel_id=1, source_target_pairs={{0,16},{2,18},{4,20},{6,22},{8,24},{10,26},{12,28},{14,30},{16,0},... | collective-permute-start | bytes 2359304 | tf_op jit(solution)/shard_map/ppermute | solution.py:12
  183.4 52.9 %all-reduce.17.cloned.1.call-start = ((), (), s32[]{:S(2)}) async-start(), calls=%async_computation.6 | async-start | bytes 524288 | tf_op jit(solution)/shard_map/psum | solution.py:34
  209.3 2.4 collective-permute-start.4
  212.8 69.4 %all-reduce.19.cloned.1.call-start = ((), (), s32[]{:S(2)}) async-start(), calls=%async_computation.7 | async-start | bytes 524288 | tf_op jit(solution)/shard_map/psum | solution.py:34
  238.7 18.8 %collective-permute-start.5 = (bf16[256,1536]{1,0:T(8,128)(2,1)S(1)}, bf16[256,1536]{1,0:T(8,128)(2,1)S(1)}, u32[]{:S(2)}, u32[]{:S(2)}) collective-permute-start(bf16[256,1536]{1,0:T(8,128)(2,1)S(1)} %fusion.20), channel_id=1, source_target_pairs={{0,4},{2,6},{4,0},{6,2},{8,12},{10,14},{12,8},{14,10},{16,20},{18,... | collective-permute-start | bytes 2359304 | tf_op jit(solution)/shard_map/ppermute | solution.py:12
  258.7 69.4 %all-reduce.21.cloned.1.call-start = ((), (), s32[]{:S(2)}) async-start(), calls=%async_computation.8 | async-start | bytes 524288 | tf_op jit(solution)/shard_map/psum | solution.py:34
  284.7 18.8 %collective-permute-start.6 = (bf16[256,1536]{1,0:T(8,128)(2,1)S(1)}, bf16[256,1536]{1,0:T(8,128)(2,1)S(1)}, u32[]{:S(2)}, u32[]{:S(2)}) collective-permute-start(bf16[256,1536]{1,0:T(8,128)(2,1)S(1)} %fusion.21), channel_id=1, source_target_pairs={{0,8},{2,10},{4,12},{6,14},{8,0},{10,2},{12,4},{14,6},{16,24},{18,... | collective-permute-start | bytes 2359304 | tf_op jit(solution)/shard_map/ppermute | solution.py:12
  304.6 87.1 %all-reduce.23.cloned.1.call-start = ((), (), s32[]{:S(2)}) async-start(), calls=%async_computation.9 | async-start | bytes 524288 | tf_op jit(solution)/shard_map/psum | solution.py:34
  330.6 36.6 %collective-permute-start.7 = (bf16[256,1536]{1,0:T(8,128)(2,1)S(1)}, bf16[256,1536]{1,0:T(8,128)(2,1)S(1)}, u32[]{:S(2)}, u32[]{:S(2)}) collective-permute-start(bf16[256,1536]{1,0:T(8,128)(2,1)S(1)} %fusion.22), channel_id=1, source_target_pairs={{0,16},{2,18},{4,20},{6,22},{8,24},{10,26},{12,28},{14,30},{16,0},... | collective-permute-start | bytes 2359304 | tf_op jit(solution)/shard_map/ppermute | solution.py:12
Sparse Core Ops, SparseCore 0:
  27.6 23.7 all-reduce.8
  73.9 23.2 all-reduce.10
  119.8 23.2 all-reduce.12
  183.5 23.2 all-reduce.14
  212.9 23.2 all-reduce.16
  258.8 23.2 all-reduce.18
  304.7 23.2 all-reduce.20
  368.4 23.2 all-reduce.22
where the time goes:
time: 417 us; the launch traced here: 416 us
  waiting for transfers between devices  330 us (79%)
  blocking collectives  27.8 us (7%)
  matrix products  20.1 us (5%)
  between operations  13.7 us (3%)
  starting transfers between devices  11.5 us (3%)
  other arithmetic  8.54 us (2%)
  local copies, waits for them, and re-layouts  4.93 us (1%)
    psum x8, waiting for transfers between devices, local(): cost = lax.psum(partial_value, 'slab') * (1.0 / math.sqrt(D))  188 us
    ppermute x8, waiting for transfers between devices, from_partner(): lax.ppermute(x, axis, [(i, i ^ 1 << stride) for i in range(lax.axis_size(...  142 us
    all_to_all x1, blocking collectives, local(): lax.all_to_all(current, 'slab', split_axis=1, concat_axis=0, tiled=True)  14.8 us
    all_to_all x1, blocking collectives, local(): lax.all_to_all(feature_part, 'slab', split_axis=0, concat_axis=1, tiled=T...  13 us
    dot_general x8, matrix products, finish_round(): aligned = 0.5 * jnp.dot(mixing, partner, preferred_element_type=jnp.float32)  11.2 us
    ppermute x8, starting transfers between devices, from_partner(): lax.ppermute(x, axis, [(i, i ^ 1 << stride) for i in range(lax.axis_size(...  11.2 us
    dot_general x8, matrix products, local(): jnp.dot(feature_part, partner.T, preferred_element_type=jnp.float32)  8.84 us
    reduce_sum x8, other arithmetic, finish_round(): soft_plan = fourth / (1.0 + jnp.sum(fourth, axis=1, keepdims=True))  8.51 us
  transfers between devices with their start and end apart: 16, of which 16 were waited for; matrix products, arithmetic and copies ran while one was open for 0% of the time, Pallas kernels for 0%

commit v1 on v0

--- a/solution.py
+++ b/solution.py
@@ -6,6 +6,11 @@
 
 D = 3072
 ROUNDS = 8
+
+
+def summed_here(shard, name):
+    blocks = lax.all_gather(shard, name)
+    return jnp.sum(blocks, axis=0)
 
 
 def from_partner(x, axis, stride):
@@ -31,7 +36,7 @@
     for round_idx in range(ROUNDS):
         partner = from_partner(feature_part, "rep", round_idx % bit_count)
         partial_value = jnp.dot(feature_part, partner.T, preferred_element_type=jnp.float32)
-        cost = lax.psum(partial_value, "slab") * (1.0 / math.sqrt(D))
+        cost = summed_here(partial_value, "slab") * (1.0 / math.sqrt(D))
         feature_part = finish_round(feature_part, partner, perm_plan[round_idx], cost)
     result = lax.all_to_all(feature_part, "slab", split_axis=0, concat_axis=1, tiled=True)
     return result[None]

time: 417 us -> 246 us (0.59)
  waiting for transfers between devices: 330 us -> 130 us
  blocking collectives: 27.8 us -> 89.3 us
  between operations: 13.7 us -> 0.29 us
  matrix products: 20.1 us -> 6.83 us
  other arithmetic: 8.54 us -> 1.22 us
    psum x8 -> x0, waiting for transfers between devices: 188 us -> none  [local(): cost = lax.psum(partial_value, 'slab') * (1.0 / math.sqrt(D))]
    all_gather x0 -> x8, blocking collectives: none -> 62.6 us  [summed_here(): blocks = lax.all_gather(shard, name)]
    ppermute x8, waiting for transfers between devices: 142 us -> 130 us  [from_partner(): lax.ppermute(x, axis, [(i, i ^ 1 << stride) for i in range(lax.axis_size(...]
    reduce_sum x8, other arithmetic: 8.51 us -> 0.92 us  [finish_round(): soft_plan = fourth / (1.0 + jnp.sum(fourth, axis=1, keepdims=True))]
    dot_general x8, matrix products: 11.2 us -> 3.66 us  [finish_round(): aligned = 0.5 * jnp.dot(mixing, partner, preferred_element_type=jnp.float32)]
    dot_general x8, matrix products: 8.84 us -> 3.17 us  [local(): jnp.dot(feature_part, partner.T, preferred_element_type=jnp.float32)]
  transfers between devices with their start and end apart: 16 -> 8, of which waited for: 16 -> 8; matrix products, arithmetic and copies ran while one was open for 0% -> 0% of each run, Pallas kernels for 0% -> 0%
where the time goes in v1:
time: 246 us
  waiting for transfers between devices  130 us (53%)
  blocking collectives  89.3 us (36%)
  starting transfers between devices  13.2 us (5%)
  matrix products  6.83 us (3%)
  local copies, waits for them, and re-layouts  4.93 us (2%)
    ppermute x8, waiting for transfers between devices, from_partner(): lax.ppermute(x, axis, [(i, i ^ 1 << stride) for i in range(lax.axis_size(...  130 us
    all_gather x8, blocking collectives, summed_here(): blocks = lax.all_gather(shard, name)  62.6 us
    all_to_all x1, blocking collectives, local(): lax.all_to_all(current, 'slab', split_axis=1, concat_axis=0, tiled=True)  14.8 us
    ppermute x8, starting transfers between devices, from_partner(): lax.ppermute(x, axis, [(i, i ^ 1 << stride) for i in range(lax.axis_size(...  13.2 us
    all_to_all x1, blocking collectives, local(): lax.all_to_all(feature_part, 'slab', split_axis=0, concat_axis=1, tiled=T...  11.9 us
  transfers between devices with their start and end apart: 8, of which 8 were waited for; matrix products, arithmetic and copies ran while one was open for 0% of the time, Pallas kernels for 0%

profile of v1, /device:TPU:0, one launch (start us, length us, event | category | flops | bytes accessed | tf_op | source)
XLA Modules:
  0.0 245.7 jit_solution(9858181487348465004)
XLA Ops:
  0.0 2.6 %all_to_all.26 = bf16[128,2,1536]{2,1,0:T(2,128)(2,1)S(1)} reshape(bf16[1,128,3072]{2,1,0:T(8,128)(2,1)} %param.2) | data formatting | bytes 1572864 | tf_op jit(solution)/shard_map/all_to_all | solution.py:35
  2.7 14.8 %all_to_all.35 = bf16[128,2,1536]{2,0,1:T(8,128)(2,1)S(1)} all-to-all(bf16[128,2,1536]{2,0,1:T(8,128)(2,1)S(1)} %copy.5), channel_id=1, replica_groups=mesh['rep'=16,'slab'=2] {'slab'}, dimensions={1} | all-to-all | bytes 1572864 | tf_op jit(solution)/shard_map/all_to_all | solution.py:35
  17.5 2.3 collective-permute-done
  20.2 9.0 %all-gather = f32[512,256]{1,0:T(8,128)S(1)} all-gather(f32[256,256]{1,0:T(8,128)S(1)} %fusion.65), channel_id=2, replica_groups=mesh['rep'=16,'slab'=2] {'slab'}, dimensions={0}, use_global_device_ids=true | all-gather | bytes 786432 | tf_op jit(solution)/shard_map/all_gather | solution.py:12
  29.4 0.5 fusion.16
  29.9 1.7 collective-permute-start.1
  31.5 17.1 %collective-permute-done.1 = bf16[256,1536]{1,0:T(8,128)(2,1)S(1)} collective-permute-done((bf16[256,1536]{1,0:T(8,128)(2,1)S(1)}, bf16[256,1536]{1,0:T(8,128)(2,1)S(1)}, u32[]{:S(2)}, u32[]{:S(2)}) %collective-permute-start.1) | collective-permute-done | bytes 786464 | tf_op jit(solution)/shard_map/ppermute | solution.py:17
  49.0 7.3 %all-gather.1 = f32[512,256]{1,0:T(8,128)S(1)} all-gather(f32[256,256]{1,0:T(8,128)S(1)} %fusion.66), channel_id=3, replica_groups=mesh['rep'=16,'slab'=2] {'slab'}, dimensions={0}, use_global_device_ids=true | all-gather | bytes 786432 | tf_op jit(solution)/shard_map/all_gather | solution.py:12
  56.5 0.5 fusion.17
  57.0 1.8 collective-permute-start.2
  58.7 15.3 %collective-permute-done.2 = bf16[256,1536]{1,0:T(8,128)(2,1)S(1)} collective-permute-done((bf16[256,1536]{1,0:T(8,128)(2,1)S(1)}, bf16[256,1536]{1,0:T(8,128)(2,1)S(1)}, u32[]{:S(2)}, u32[]{:S(2)}) %collective-permute-start.2) | collective-permute-done | bytes 786464 | tf_op jit(solution)/shard_map/ppermute | solution.py:17
  74.5 7.0 %all-gather.2 = f32[512,256]{1,0:T(8,128)S(1)} all-gather(f32[256,256]{1,0:T(8,128)S(1)} %fusion.67), channel_id=4, replica_groups=mesh['rep'=16,'slab'=2] {'slab'}, dimensions={0}, use_global_device_ids=true | all-gather | bytes 786432 | tf_op jit(solution)/shard_map/all_gather | solution.py:12
  82.1 2.8 %collective-permute-start.3 = (bf16[256,1536]{1,0:T(8,128)(2,1)S(1)}, bf16[256,1536]{1,0:T(8,128)(2,1)S(1)}, u32[]{:S(2)}, u32[]{:S(2)}) collective-permute-start(bf16[256,1536]{1,0:T(8,128)(2,1)S(1)} %fusion.18), channel_id=1, source_target_pairs={{0,16},{2,18},{4,20},{6,22},{8,24},{10,26},{12,28},{14,30},{16,0},... | collective-permute-start | bytes 2359304 | tf_op jit(solution)/shard_map/ppermute | solution.py:17
  84.9 30.1 %collective-permute-done.3 = bf16[256,1536]{1,0:T(8,128)(2,1)S(1)} collective-permute-done((bf16[256,1536]{1,0:T(8,128)(2,1)S(1)}, bf16[256,1536]{1,0:T(8,128)(2,1)S(1)}, u32[]{:S(2)}, u32[]{:S(2)}) %collective-permute-start.3) | collective-permute-done | bytes 786464 | tf_op jit(solution)/shard_map/ppermute | solution.py:17
  115.4 7.9 %all-gather.3 = f32[512,256]{1,0:T(8,128)S(1)} all-gather(f32[256,256]{1,0:T(8,128)S(1)} %fusion.68), channel_id=5, replica_groups=mesh['rep'=16,'slab'=2] {'slab'}, dimensions={0}, use_global_device_ids=true | all-gather | bytes 786432 | tf_op jit(solution)/shard_map/all_gather | solution.py:12
  123.4 0.5 fusion.19
  124.0 2.3 collective-permute-done.4
  126.7 9.0 %all-gather.4 = f32[512,256]{1,0:T(8,128)S(1)} all-gather(f32[256,256]{1,0:T(8,128)S(1)} %fusion.69), channel_id=6, replica_groups=mesh['rep'=16,'slab'=2] {'slab'}, dimensions={0}, use_global_device_ids=true | all-gather | bytes 786432 | tf_op jit(solution)/shard_map/all_gather | solution.py:12
  136.3 1.6 collective-permute-start.5
  137.9 17.2 %collective-permute-done.5 = bf16[256,1536]{1,0:T(8,128)(2,1)S(1)} collective-permute-done((bf16[256,1536]{1,0:T(8,128)(2,1)S(1)}, bf16[256,1536]{1,0:T(8,128)(2,1)S(1)}, u32[]{:S(2)}, u32[]{:S(2)}) %collective-permute-start.5) | collective-permute-done | bytes 786464 | tf_op jit(solution)/shard_map/ppermute | solution.py:17
  155.5 7.3 %all-gather.5 = f32[512,256]{1,0:T(8,128)S(1)} all-gather(f32[256,256]{1,0:T(8,128)S(1)} %fusion.70), channel_id=7, replica_groups=mesh['rep'=16,'slab'=2] {'slab'}, dimensions={0}, use_global_device_ids=true | all-gather | bytes 786432 | tf_op jit(solution)/shard_map/all_gather | solution.py:12
  163.0 0.5 fusion.21
  163.5 1.8 collective-permute-start.6
  165.3 15.3 %collective-permute-done.6 = bf16[256,1536]{1,0:T(8,128)(2,1)S(1)} collective-permute-done((bf16[256,1536]{1,0:T(8,128)(2,1)S(1)}, bf16[256,1536]{1,0:T(8,128)(2,1)S(1)}, u32[]{:S(2)}, u32[]{:S(2)}) %collective-permute-start.6) | collective-permute-done | bytes 786464 | tf_op jit(solution)/shard_map/ppermute | solution.py:17
  181.0 7.0 %all-gather.6 = f32[512,256]{1,0:T(8,128)S(1)} all-gather(f32[256,256]{1,0:T(8,128)S(1)} %fusion.71), channel_id=8, replica_groups=mesh['rep'=16,'slab'=2] {'slab'}, dimensions={0}, use_global_device_ids=true | all-gather | bytes 786432 | tf_op jit(solution)/shard_map/all_gather | solution.py:12
  188.6 3.4 %collective-permute-start.7 = (bf16[256,1536]{1,0:T(8,128)(2,1)S(1)}, bf16[256,1536]{1,0:T(8,128)(2,1)S(1)}, u32[]{:S(2)}, u32[]{:S(2)}) collective-permute-start(bf16[256,1536]{1,0:T(8,128)(2,1)S(1)} %fusion.22), channel_id=1, source_target_pairs={{0,16},{2,18},{4,20},{6,22},{8,24},{10,26},{12,28},{14,30},{16,0},... | collective-permute-start | bytes 2359304 | tf_op jit(solution)/shard_map/ppermute | solution.py:17
  192.1 30.4 %collective-permute-done.7 = bf16[256,1536]{1,0:T(8,128)(2,1)S(1)} collective-permute-done((bf16[256,1536]{1,0:T(8,128)(2,1)S(1)}, bf16[256,1536]{1,0:T(8,128)(2,1)S(1)}, u32[]{:S(2)}, u32[]{:S(2)}) %collective-permute-start.7) | collective-permute-done | bytes 786464 | tf_op jit(solution)/shard_map/ppermute | solution.py:17
  222.8 8.0 %all-gather.7 = f32[512,256]{1,0:T(8,128)S(1)} all-gather(f32[256,256]{1,0:T(8,128)S(1)} %fusion.72), channel_id=9, replica_groups=mesh['rep'=16,'slab'=2] {'slab'}, dimensions={0}, use_global_device_ids=true | all-gather | bytes 786432 | tf_op jit(solution)/shard_map/all_gather | solution.py:12
  231.0 0.5 fusion.23
  231.5 11.9 %all_to_all.36 = bf16[2,128,1536]{2,1,0:T(8,128)(2,1)S(1)} all-to-all(bf16[2,128,1536]{2,1,0:T(8,128)(2,1)S(1)} %bitcast.57), channel_id=1, replica_groups=mesh['rep'=16,'slab'=2] {'slab'}, dimensions={0} | all-to-all | bytes 1572864 | tf_op jit(solution)/shard_map/all_to_all | solution.py:41
  243.4 0.8 copy.6
  244.2 1.5 broadcast_in_dim.2
  (41 shorter events, 5.9 us)
Async XLA Ops:
  2.7 14.9 %copy-start = (s32[1,8,256]{2,1,0:T(8,128)S(1)}, s32[1,8,256]{2,1,0:T(8,128)}, u32[]{:S(2)}) copy-start(s32[1,8,256]{2,1,0:T(8,128)} %param.3) | copy-start | bytes 24580
  17.5 2.3 collective-permute-start
  29.9 18.8 %collective-permute-start.1 = (bf16[256,1536]{1,0:T(8,128)(2,1)S(1)}, bf16[256,1536]{1,0:T(8,128)(2,1)S(1)}, u32[]{:S(2)}, u32[]{:S(2)}) collective-permute-start(bf16[256,1536]{1,0:T(8,128)(2,1)S(1)} %fusion.16), channel_id=1, source_target_pairs={{0,4},{2,6},{4,0},{6,2},{8,12},{10,14},{12,8},{14,10},{16,20},{18,... | collective-permute-start | bytes 2359304 | tf_op jit(solution)/shard_map/ppermute | solution.py:17
  57.0 17.1 %collective-permute-start.2 = (bf16[256,1536]{1,0:T(8,128)(2,1)S(1)}, bf16[256,1536]{1,0:T(8,128)(2,1)S(1)}, u32[]{:S(2)}, u32[]{:S(2)}) collective-permute-start(bf16[256,1536]{1,0:T(8,128)(2,1)S(1)} %fusion.17), channel_id=1, source_target_pairs={{0,8},{2,10},{4,12},{6,14},{8,0},{10,2},{12,4},{14,6},{16,24},{18,... | collective-permute-start | bytes 2359304 | tf_op jit(solution)/shard_map/ppermute | solution.py:17
  82.1 32.9 %collective-permute-start.3 = (bf16[256,1536]{1,0:T(8,128)(2,1)S(1)}, bf16[256,1536]{1,0:T(8,128)(2,1)S(1)}, u32[]{:S(2)}, u32[]{:S(2)}) collective-permute-start(bf16[256,1536]{1,0:T(8,128)(2,1)S(1)} %fusion.18), channel_id=1, source_target_pairs={{0,16},{2,18},{4,20},{6,22},{8,24},{10,26},{12,28},{14,30},{16,0},... | collective-permute-start | bytes 2359304 | tf_op jit(solution)/shard_map/ppermute | solution.py:17
  123.9 2.4 collective-permute-start.4
  136.3 18.8 %collective-permute-start.5 = (bf16[256,1536]{1,0:T(8,128)(2,1)S(1)}, bf16[256,1536]{1,0:T(8,128)(2,1)S(1)}, u32[]{:S(2)}, u32[]{:S(2)}) collective-permute-start(bf16[256,1536]{1,0:T(8,128)(2,1)S(1)} %fusion.20), channel_id=1, source_target_pairs={{0,4},{2,6},{4,0},{6,2},{8,12},{10,14},{12,8},{14,10},{16,20},{18,... | collective-permute-start | bytes 2359304 | tf_op jit(solution)/shard_map/ppermute | solution.py:17
  163.5 17.1 %collective-permute-start.6 = (bf16[256,1536]{1,0:T(8,128)(2,1)S(1)}, bf16[256,1536]{1,0:T(8,128)(2,1)S(1)}, u32[]{:S(2)}, u32[]{:S(2)}) collective-permute-start(bf16[256,1536]{1,0:T(8,128)(2,1)S(1)} %fusion.21), channel_id=1, source_target_pairs={{0,8},{2,10},{4,12},{6,14},{8,0},{10,2},{12,4},{14,6},{16,24},{18,... | collective-permute-start | bytes 2359304 | tf_op jit(solution)/shard_map/ppermute | solution.py:17
  188.6 33.8 %collective-permute-start.7 = (bf16[256,1536]{1,0:T(8,128)(2,1)S(1)}, bf16[256,1536]{1,0:T(8,128)(2,1)S(1)}, u32[]{:S(2)}, u32[]{:S(2)}) collective-permute-start(bf16[256,1536]{1,0:T(8,128)(2,1)S(1)} %fusion.22), channel_id=1, source_target_pairs={{0,16},{2,18},{4,20},{6,22},{8,24},{10,26},{12,28},{14,30},{16,0},... | collective-permute-start | bytes 2359304 | tf_op jit(solution)/shard_map/ppermute | solution.py:17
